TPU v7x, 32 devices: a whole 2x2x4 slice. The times are simulated.
32 devices in a mesh: cand: 4 (over x, core), tp: 8 (over z, y).
Axes of the slice: x: 2, y: 2, z: 4, core: 2. Of those that a mesh axis runs over, the one named last changes fastest.
Arguments:
- start_state: float32 [128], replicated, may hold values from -6 to 6
- goal: float32 [128], replicated, may hold values from -6 to 6
- mean_prev: float32 [128], replicated, may hold values from -0.5 to 0.5
- std_prev: float32 [128], replicated, may hold values from 0.1 to 0.5
- noise: float32 [768, 128], P('cand'), may hold values from -23 to 23
- members: int32 [768, 1], P('cand'), may hold values from 0 to 3; in each aligned block of 192 rows (0 to 191, 192 to 383, ...) at most 60 rows name the same one
- elites: int32 [96], replicated, may hold values from 0 to 767, as said below
- w_in: bfloat16 [4, 144, 4096], P(None, None, 'tp'), may hold values from -0.5 to 0.5
- w_hid: bfloat16 [4, 4096, 4096], P(None, None, 'tp'), may hold values from -0.09375 to 0.09375
- w_out: bfloat16 [4, 4096, 128], P(None, 'tp'), may hold values from -0.09375 to 0.09375
Outputs:
- scores: float32 [768], P('cand')
- new_mean: float32 [128], replicated
- new_std: float32 [128], replicated
Inputs may be any that keep to these rules, and one draw needn't show every extreme that they name: `members`: among the candidates of one index of cand no member is named more than 60 times. `elites`: 96 distinct candidate numbers.
All inputs are finite; a program needn't handle non-finite values.
Results may differ from a plain program's by a relative error of at most 0.0085.
Values may be sent and summed in bfloat16 or wider, within the bound.
A program may use at most 64 MiB of HBM per device.

v0:
```python
import jax
import jax.numpy as jnp
from jax import lax
from jax.sharding import PartitionSpec as P

HORIZON = 8


def reward_of(states, goal, action):
    return -jnp.mean((states - goal) ** 2, axis=-1) - 0.1 * jnp.mean(action * action, axis=-1)


def on_device(start_state, goal, mean_prev, std_prev, noise, members, elites, w_in, w_hid, w_out):
    local_count = noise.shape[0]
    member_count = w_in.shape[0]
    state_width = start_state.shape[0]
    capacity = 5 * local_count // 16
    action_width = mean_prev.shape[0] // HORIZON
    actions = mean_prev[None, :] + std_prev[None, :] * noise
    onehot = (members == jnp.arange(member_count, dtype=jnp.int32)[None, :]).astype(jnp.float32)
    before = jnp.cumsum(onehot, axis=0) - onehot
    position = jnp.sum(before * onehot, axis=1).astype(jnp.int32)
    slot_number = members[:, 0] * capacity + position
    dispatch = (
        slot_number[None, :] == jnp.arange(member_count * capacity, dtype=jnp.int32)[:, None]
    ).astype(jnp.float32)
    slot_actions = jnp.dot(dispatch, actions, precision=lax.Precision.HIGHEST)
    slot_actions = slot_actions.reshape(member_count, capacity, HORIZON, action_width)
    input_layer = lax.all_gather(w_in, "tp", axis=2, tiled=True)

    def rollout(first, count):
        layer_in = input_layer[first : first + count]
        hid_rows = w_hid[first : first + count]
        out_rows = w_out[first : first + count]
        states = jnp.zeros((count, capacity, state_width), jnp.float32) + start_state[None, None, :]
        running = jnp.zeros((count, capacity), jnp.float32)
        for step_index in range(HORIZON):
            action = slot_actions[first : first + count, :, step_index, :]
            inputs = jnp.concatenate([states, action], axis=2).astype(jnp.bfloat16)
            first_pre = jnp.einsum(
                "mck,mkh->mch", inputs, layer_in, preferred_element_type=jnp.float32
            )
            hidden_one = jax.nn.silu(first_pre).astype(jnp.bfloat16)
            second_pre = jnp.einsum(
                "mck,mkh->mch", hidden_one, hid_rows, preferred_element_type=jnp.float32
            )
            hidden_two = jax.nn.silu(second_pre).astype(jnp.bfloat16)
            partial_change = jnp.einsum(
                "mck,mks->mcs", hidden_two, out_rows, preferred_element_type=jnp.float32
            )
            change = lax.psum(partial_change, "tp")
            states = states + change
            running = running + reward_of(states, goal[None, None, :], action)
        return running

    slot_returns = jnp.concatenate([rollout(member, 1) for member in range(member_count)], axis=0)
    returns = jnp.dot(
        slot_returns.reshape(member_count * capacity), dispatch, precision=lax.Precision.HIGHEST
    )
    first_index = lax.axis_index("cand") * local_count
    numbers = first_index + jnp.arange(local_count, dtype=jnp.int32)
    chosen = jnp.sum((elites[:, None] == numbers[None, :]).astype(jnp.float32), axis=0)
    count_all = local_count * lax.axis_size("cand")
    return_sum = lax.psum(jnp.sum(returns), "cand")
    return_mean = return_sum / count_all
    return_spread = lax.psum(jnp.sum((returns - return_mean) ** 2), "cand")
    return_var = return_spread / count_all
    scores = (returns - return_mean) / jnp.sqrt(return_var + 1e-06)
    weights = chosen * (0.5 + jax.nn.sigmoid(scores))
    weight_sum, first_moment = lax.psum(
        (jnp.sum(weights), jnp.dot(weights, actions, precision=lax.Precision.HIGHEST)), "cand"
    )
    new_mean = first_moment / weight_sum
    action_spread = lax.psum(
        jnp.dot(weights, (actions - new_mean[None, :]) ** 2, precision=lax.Precision.HIGHEST),
        "cand",
    )
    new_var = action_spread / weight_sum
    new_std = jnp.sqrt(new_var + 1e-06)
    return (scores, new_mean, new_std)


def solution(mesh):
    placed = (
        P(),
        P(),
        P(),
        P(),
        P("cand", None),
        P("cand", None),
        P(),
        P(None, None, "tp"),
        P(None, None, "tp"),
        P(None, "tp", None),
    )
    return jax.shard_map(
        on_device, mesh=mesh, in_specs=placed, out_specs=(P("cand"), P(), P()), check_vma=False
    )
```

profile of v0, /device:TPU:0, one launch (start us, length us, event | category | flops | bytes accessed | tf_op | source)
XLA Modules:
  0.0 847.4 jit_solution(5525363201203804489)
XLA Ops:
  16.0 77.4 %all-gather.2.cloned.1.call-done = bf16[4,144,4096]{2,1,0:T(8,128)(2,1)} async-done(((bf16[4,144,512]{2,1,0:T(8,128)(2,1)}), bf16[4,144,4096]{2,1,0:T(8,128)(2,1)}) %all-gather.2.cloned.1.call-update) | async-done | bytes 4718608 | tf_op jit(solution)/shard_map/all_gather | solution.py:29
  93.4 3.7 multiply_convert_fusion.109
  106.8 3.7 multiply_convert_fusion.85
  111.8 69.2 %all-reduce.33.cloned.1.call-done = (f32[1,60,128]{2,1,0:T(8,128)}, f32[1,60,128]{2,1,0:T(8,128)}, f32[1,60,128]{2,1,0:T(8,128)}, f32[1,60,128]{2,1,0:T(8,128)}) async-done(((f32[1,60,128]{2,1,0:T(8,128)}, f32[1,60,128]{2,1,0:T(8,128)}, f32[1,60,128]{2,1,0:T(8,128)}, f32[1,60,128]{2,1,0:T(8,128)}), (f32[1,60,128]{2,1,0:T(8,128)}, f32[1,60,128]{2,1,0:T(8,128)}, f32[1,60,128]{2,1,0:T(8,128)}, ...) | async-done | bytes 122896 | tf_op jit(solution)/shard_map/psum | solution.py:51
  195.1 3.7 multiply_convert_fusion.130
  200.4 69.7 %all-reduce.31.cloned.1.call-done = (f32[1,60,128]{2,1,0:T(8,128)}, f32[1,60,128]{2,1,0:T(8,128)}, f32[1,60,128]{2,1,0:T(8,128)}, f32[1,60,128]{2,1,0:T(8,128)}) async-done(((f32[1,60,128]{2,1,0:T(8,128)}, f32[1,60,128]{2,1,0:T(8,128)}, f32[1,60,128]{2,1,0:T(8,128)}, f32[1,60,128]{2,1,0:T(8,128)}), (f32[1,60,128]{2,1,0:T(8,128)}, f32[1,60,128]{2,1,0:T(8,128)}, f32[1,60,128]{2,1,0:T(8,128)}, ...) | async-done | bytes 122896 | tf_op jit(solution)/shard_map/psum | solution.py:51
  271.0 3.7 multiply_convert_fusion.151
  289.5 69.9 %all-reduce.29.cloned.1.call-done = (f32[1,60,128]{2,1,0:T(8,128)}, f32[1,60,128]{2,1,0:T(8,128)}, f32[1,60,128]{2,1,0:T(8,128)}, f32[1,60,128]{2,1,0:T(8,128)}) async-done(((f32[1,60,128]{2,1,0:T(8,128)}, f32[1,60,128]{2,1,0:T(8,128)}, f32[1,60,128]{2,1,0:T(8,128)}, f32[1,60,128]{2,1,0:T(8,128)}), (f32[1,60,128]{2,1,0:T(8,128)}, f32[1,60,128]{2,1,0:T(8,128)}, f32[1,60,128]{2,1,0:T(8,128)}, ...) | async-done | bytes 122896 | tf_op jit(solution)/shard_map/psum | solution.py:51
  360.2 3.7 multiply_convert_fusion.148
  373.6 3.7 multiply_convert_fusion.124
  378.8 69.9 %all-reduce.27.cloned.1.call-done = (f32[1,60,128]{2,1,0:T(8,128)}, f32[1,60,128]{2,1,0:T(8,128)}, f32[1,60,128]{2,1,0:T(8,128)}, f32[1,60,128]{2,1,0:T(8,128)}) async-done(((f32[1,60,128]{2,1,0:T(8,128)}, f32[1,60,128]{2,1,0:T(8,128)}, f32[1,60,128]{2,1,0:T(8,128)}, f32[1,60,128]{2,1,0:T(8,128)}), (f32[1,60,128]{2,1,0:T(8,128)}, f32[1,60,128]{2,1,0:T(8,128)}, f32[1,60,128]{2,1,0:T(8,128)}, ...) | async-done | bytes 122896 | tf_op jit(solution)/shard_map/psum | solution.py:51
  458.4 3.7 multiply_convert_fusion.97
  462.9 3.7 multiply_convert_fusion.121
  468.3 69.7 %all-reduce.25.cloned.1.call-done = (f32[1,60,128]{2,1,0:T(8,128)}, f32[1,60,128]{2,1,0:T(8,128)}, f32[1,60,128]{2,1,0:T(8,128)}, f32[1,60,128]{2,1,0:T(8,128)}) async-done(((f32[1,60,128]{2,1,0:T(8,128)}, f32[1,60,128]{2,1,0:T(8,128)}, f32[1,60,128]{2,1,0:T(8,128)}, f32[1,60,128]{2,1,0:T(8,128)}), (f32[1,60,128]{2,1,0:T(8,128)}, f32[1,60,128]{2,1,0:T(8,128)}, f32[1,60,128]{2,1,0:T(8,128)}, ...) | async-done | bytes 122896 | tf_op jit(solution)/shard_map/psum | solution.py:51
  538.7 3.7 multiply_convert_fusion.142
  543.2 3.7 multiply_convert_fusion.70
  547.7 3.7 multiply_convert_fusion.94
  552.2 3.7 multiply_convert_fusion.118
  557.2 70.0 %all-reduce.23.cloned.1.call-done = (f32[1,60,128]{2,1,0:T(8,128)}, f32[1,60,128]{2,1,0:T(8,128)}, f32[1,60,128]{2,1,0:T(8,128)}, f32[1,60,128]{2,1,0:T(8,128)}) async-done(((f32[1,60,128]{2,1,0:T(8,128)}, f32[1,60,128]{2,1,0:T(8,128)}, f32[1,60,128]{2,1,0:T(8,128)}, f32[1,60,128]{2,1,0:T(8,128)}), (f32[1,60,128]{2,1,0:T(8,128)}, f32[1,60,128]{2,1,0:T(8,128)}, f32[1,60,128]{2,1,0:T(8,128)}, ...) | async-done | bytes 122896 | tf_op jit(solution)/shard_map/psum | solution.py:51
  628.0 3.7 multiply_convert_fusion.139
  632.5 3.7 multiply_convert_fusion.67
  641.4 3.7 multiply_convert_fusion.115
  646.1 70.3 %all-reduce.21.cloned.1.call-done = (f32[1,60,128]{2,1,0:T(8,128)}, f32[1,60,128]{2,1,0:T(8,128)}, f32[1,60,128]{2,1,0:T(8,128)}, f32[1,60,128]{2,1,0:T(8,128)}) async-done(((f32[1,60,128]{2,1,0:T(8,128)}, f32[1,60,128]{2,1,0:T(8,128)}, f32[1,60,128]{2,1,0:T(8,128)}, f32[1,60,128]{2,1,0:T(8,128)}), (f32[1,60,128]{2,1,0:T(8,128)}, f32[1,60,128]{2,1,0:T(8,128)}, f32[1,60,128]{2,1,0:T(8,128)}, ...) | async-done | bytes 122896 | tf_op jit(solution)/shard_map/psum | solution.py:51
  717.2 3.7 multiply_convert_fusion.136
  721.7 3.7 multiply_convert_fusion.64
  726.2 3.7 multiply_convert_fusion.88
  730.7 3.7 multiply_convert_fusion.112
  735.2 70.5 %all-reduce.19.cloned.1.call-done = (f32[1,60,128]{2,1,0:T(8,128)}, f32[1,60,128]{2,1,0:T(8,128)}, f32[1,60,128]{2,1,0:T(8,128)}, f32[1,60,128]{2,1,0:T(8,128)}) async-done(((f32[1,60,128]{2,1,0:T(8,128)}, f32[1,60,128]{2,1,0:T(8,128)}, f32[1,60,128]{2,1,0:T(8,128)}, f32[1,60,128]{2,1,0:T(8,128)}), (f32[1,60,128]{2,1,0:T(8,128)}, f32[1,60,128]{2,1,0:T(8,128)}, f32[1,60,128]{2,1,0:T(8,128)}, ...) | async-done | bytes 122896 | tf_op jit(solution)/shard_map/psum | solution.py:51
  809.2 6.3 psum.291
  816.8 7.2 psum.292
  826.1 6.6 all-reduce.9
  833.6 6.0 psum.295
  (225 shorter events, 98.6 us)
Async XLA Ops:
  7.2 86.2 %all-gather.2.cloned.1.call-start = ((), (), s32[]{:S(2)}) async-start(), calls=%async_computation | async-start | bytes 5308416 | tf_op jit(solution)/shard_map/all_gather | solution.py:29
  7.9 173.0 %all-reduce.33.cloned.1.call-start = ((), (), s32[]{:S(2)}) async-start(), calls=%async_computation.8 | async-start | bytes 262144 | tf_op jit(solution)/shard_map/psum | solution.py:51
  106.8 74.1 %copy-start.22 = (f32[128]{0:T(128)S(1)}, f32[128]{0:T(128)}, u32[]{:S(2)}) copy-start(f32[128]{0:T(128)} %param.10) | copy-start | bytes 1540
  111.3 158.8 %all-reduce.31.cloned.1.call-start = ((), (), s32[]{:S(2)}) async-start(), calls=%async_computation.7 | async-start | bytes 262144 | tf_op jit(solution)/shard_map/psum | solution.py:51
  195.1 75.0 %copy-start.2 = (f32[1,60,128]{2,1,0:T(8,128)S(1)}, f32[1,60,128]{2,1,0:T(8,128)}, u32[]{:S(2)}) copy-start(f32[1,60,128]{2,1,0:T(8,128)} %get-tuple-element.73) | copy-start | bytes 92164
  195.1 75.0 %copy-start.3 = (f32[1,60,128]{2,1,0:T(8,128)S(1)}, f32[1,60,128]{2,1,0:T(8,128)}, u32[]{:S(2)}) copy-start(f32[1,60,128]{2,1,0:T(8,128)} %get-tuple-element.74) | copy-start | bytes 92164
  195.1 75.0 %copy-start.4 = (f32[1,60,128]{2,1,0:T(8,128)S(1)}, f32[1,60,128]{2,1,0:T(8,128)}, u32[]{:S(2)}) copy-start(f32[1,60,128]{2,1,0:T(8,128)} %get-tuple-element.75) | copy-start | bytes 92164
  195.1 75.0 %copy-start.5 = (f32[1,60,128]{2,1,0:T(8,128)S(1)}, f32[1,60,128]{2,1,0:T(8,128)}, u32[]{:S(2)}) copy-start(f32[1,60,128]{2,1,0:T(8,128)} %get-tuple-element.76) | copy-start | bytes 92164
  199.6 159.8 %all-reduce.29.cloned.1.call-start = ((), (), s32[]{:S(2)}) async-start(), calls=%async_computation.6 | async-start | bytes 262144 | tf_op jit(solution)/shard_map/psum | solution.py:51
  288.9 159.8 %all-reduce.27.cloned.1.call-start = ((), (), s32[]{:S(2)}) async-start(), calls=%async_computation.5 | async-start | bytes 262144 | tf_op jit(solution)/shard_map/psum | solution.py:51
  360.2 4.5 copy-start.12
  360.2 4.5 copy-start.13
  378.1 159.8 %all-reduce.25.cloned.1.call-start = ((), (), s32[]{:S(2)}) async-start(), calls=%async_computation.4 | async-start | bytes 262144 | tf_op jit(solution)/shard_map/psum | solution.py:51
  449.4 4.5 copy-start.17
  453.9 4.5 copy-start.11
  458.4 4.5 copy-start.8
  467.4 159.8 %all-reduce.23.cloned.1.call-start = ((), (), s32[]{:S(2)}) async-start(), calls=%async_computation.3 | async-start | bytes 262144 | tf_op jit(solution)/shard_map/psum | solution.py:51
  538.7 4.5 copy-start.15
  543.2 4.5 copy-start.9
  547.7 4.5 copy-start.6
  556.7 159.7 %all-reduce.21.cloned.1.call-start = ((), (), s32[]{:S(2)}) async-start(), calls=%async_computation.2 | async-start | bytes 262144 | tf_op jit(solution)/shard_map/psum | solution.py:51
  632.5 4.5 copy-start.10
  637.0 4.5 copy-start.7
  645.9 159.8 %all-reduce.19.cloned.1.call-start = ((), (), s32[]{:S(2)}) async-start(), calls=%async_computation.1 | async-start | bytes 262144 | tf_op jit(solution)/shard_map/psum | solution.py:51
  721.7 4.5 copy-start.18
  726.2 4.5 copy-start.14
  730.7 75.1 %copy-start.23 = (f32[128]{0:T(128)S(1)}, f32[128]{0:T(128)}, u32[]{:S(2)}) copy-start(f32[128]{0:T(128)} %param.11) | copy-start | bytes 1540
  730.7 86.1 %copy-start.25 = (s32[96]{0:T(128)S(1)}, s32[96]{0:T(128)}, u32[]{:S(2)}) copy-start(s32[96]{0:T(128)} %param.16) | copy-start | bytes 1156
  730.7 95.3 %copy-start.1 = (f32[192,128]{1,0:T(8,128)S(1)}, f32[192,128]{1,0:T(8,128)}, u32[]{:S(2)}) copy-start(f32[192,128]{1,0:T(8,128)} %param.14) | copy-start | bytes 294916
  730.7 95.2 %copy-start.20 = (f32[128]{0:T(128)S(1)}, f32[128]{0:T(128)}, u32[]{:S(2)}) copy-start(f32[128]{0:T(128)} %param.13) | copy-start | bytes 1540
  730.7 95.2 %copy-start.21 = (f32[128]{0:T(128)S(1)}, f32[128]{0:T(128)}, u32[]{:S(2)}) copy-start(f32[128]{0:T(128)} %param.12) | copy-start | bytes 1540
  833.4 7.4 copy-start.24
  (3 other events, 12.7 us)
Sparse Core Ops, SparseCore 0:
  10.0 83.3 all-gather.1
  111.4 69.4 all-reduce.32
  199.8 70.3 all-reduce.30
  289.0 70.3 all-reduce.28
  378.3 70.3 all-reduce.26
  467.5 70.4 all-reduce.24
  556.8 70.3 all-reduce.22
  646.1 70.3 all-reduce.20
  735.4 70.3 all-reduce.18
where the time goes:
time: 849 us; the launch traced here: 847 us
  waiting for transfers between devices  637 us (75%)
  matrix products  144 us (17%)
  blocking collectives  26.2 us (3%)
  other arithmetic  19 us (2%)
  between operations  15.8 us (2%)
    psum x8, waiting for transfers between devices, rollout(): change = lax.psum(partial_change, 'tp')  559 us
    dot_general x32, matrix products, rollout(): jnp.einsum('mck,mkh->mch', hidden_one, hid_rows, preferred_element_type=j...  118 us
    all_gather x1, waiting for transfers between devices, on_device(): input_layer = lax.all_gather(w_in, 'tp', axis=2, tiled=True)  77.4 us
    dot_general x32, matrix products, rollout(): jnp.einsum('mck,mks->mcs', hidden_two, out_rows, preferred_element_type=j...  24.4 us
  transfers between devices with their start and end apart: 9, of which 9 were waited for; matrix products, arithmetic and copies ran while one was open for 1% of the time, Pallas kernels for 0%

commit v1 on v0

--- a/solution.py
+++ b/solution.py
@@ -48,7 +48,7 @@
             partial_change = jnp.einsum(
                 "mck,mks->mcs", hidden_two, out_rows, preferred_element_type=jnp.float32
             )
-            change = lax.psum(partial_change, "tp")
+            change = jnp.sum(lax.all_gather(partial_change, "tp"), axis=0)
             states = states + change
             running = running + reward_of(states, goal[None, None, :], action)
         return running

time: 849 us -> 1260 us (1.48)
  blocking collectives: 26.2 us -> 1010 us
  waiting for transfers between devices: 637 us -> 76.1 us
  matrix products: 144 us -> 125 us
    all_gather x0 -> x32, blocking collectives: none -> 987 us  [rollout(): change = jnp.sum(lax.all_gather(partial_change, 'tp'), axis=0)]
    psum x8 -> x0, waiting for transfers between devices: 559 us -> none  [rollout(): change = lax.psum(partial_change, 'tp')]
    dot_general x32, matrix products: 24.4 us -> 4.88 us  [rollout(): jnp.einsum('mck,mks->mcs', hidden_two, out_rows, preferred_element_type=j...]
  transfers between devices with their start and end apart: 9 -> 1, of which waited for: 9 -> 1; matrix products, arithmetic and copies ran while one was open for 1% -> 1% of each run, Pallas kernels for 0% -> 0%
where the time goes in v1:
time: 1260 us; the launch traced here: 1250 us
  blocking collectives  1010 us (80%)
  matrix products  125 us (10%)
  waiting for transfers between devices  76.1 us (6%)
  between operations  16.4 us (1%)
    all_gather x32, blocking collectives, rollout(): change = jnp.sum(lax.all_gather(partial_change, 'tp'), axis=0)  987 us
    dot_general x32, matrix products, rollout(): jnp.einsum('mck,mkh->mch', hidden_one, hid_rows, preferred_element_type=j...  118 us
    all_gather x1, waiting for transfers between devices, on_device(): input_layer = lax.all_gather(w_in, 'tp', axis=2, tiled=True)  75.4 us
  transfers between devices with their start and end apart: 1, of which 1 were waited for; matrix products, arithmetic and copies ran while one was open for 1% of the time, Pallas kernels for 0%

profile of v1, /device:TPU:0, one launch (start us, length us, event | category | flops | bytes accessed | tf_op | source)
XLA Modules:
  0.0 1246.3 jit_solution(15353539271136131897)
XLA Ops:
  18.0 75.4 %all-gather.66.cloned.1.call-done = bf16[4,144,4096]{2,1,0:T(8,128)(2,1)} async-done(((bf16[4,144,512]{2,1,0:T(8,128)(2,1)}), bf16[4,144,4096]{2,1,0:T(8,128)(2,1)}) %all-gather.66.cloned.1.call-update) | async-done | bytes 4718608 | tf_op jit(solution)/shard_map/all_gather | solution.py:29
  108.9 30.9 %all-gather.40 = f32[8,60,128]{2,1,0:T(8,128)S(1)} all-gather(f32[1,60,128]{2,1,0:T(8,128)S(1)} %convolution_bitcast_fusion.23), channel_id=10, replica_groups=mesh['cand'=4,'tp'=8] {'tp'}, dimensions={0}, use_global_device_ids=true | all-gather | bytes 276480 | tf_op jit(solution)/shard_map/all_gather | solution.py:51
  139.8 31.0 %all-gather.32 = f32[8,60,128]{2,1,0:T(8,128)S(1)} all-gather(f32[1,60,128]{2,1,0:T(8,128)S(1)} %convolution_bitcast_fusion.31), channel_id=2, replica_groups=mesh['cand'=4,'tp'=8] {'tp'}, dimensions={0}, use_global_device_ids=true | all-gather | bytes 276480 | tf_op jit(solution)/shard_map/all_gather | solution.py:51
  178.6 31.1 %all-gather.33 = f32[8,60,128]{2,1,0:T(8,128)S(1)} all-gather(f32[1,60,128]{2,1,0:T(8,128)S(1)} %convolution_bitcast_fusion.30), channel_id=3, replica_groups=mesh['cand'=4,'tp'=8] {'tp'}, dimensions={0}, use_global_device_ids=true | all-gather | bytes 276480 | tf_op jit(solution)/shard_map/all_gather | solution.py:51
  209.7 31.0 %all-gather.41 = f32[8,60,128]{2,1,0:T(8,128)S(1)} all-gather(f32[1,60,128]{2,1,0:T(8,128)S(1)} %convolution_bitcast_fusion.22), channel_id=11, replica_groups=mesh['cand'=4,'tp'=8] {'tp'}, dimensions={0}, use_global_device_ids=true | all-gather | bytes 276480 | tf_op jit(solution)/shard_map/all_gather | solution.py:51
  240.7 31.0 %all-gather.56 = f32[8,60,128]{2,1,0:T(8,128)S(1)} all-gather(f32[1,60,128]{2,1,0:T(8,128)S(1)} %convolution_bitcast_fusion.7), channel_id=26, replica_groups=mesh['cand'=4,'tp'=8] {'tp'}, dimensions={0}, use_global_device_ids=true | all-gather | bytes 276480 | tf_op jit(solution)/shard_map/all_gather | solution.py:51
  271.7 30.8 %all-gather.48 = f32[8,60,128]{2,1,0:T(8,128)S(1)} all-gather(f32[1,60,128]{2,1,0:T(8,128)S(1)} %convolution_bitcast_fusion.15), channel_id=18, replica_groups=mesh['cand'=4,'tp'=8] {'tp'}, dimensions={0}, use_global_device_ids=true | all-gather | bytes 276480 | tf_op jit(solution)/shard_map/all_gather | solution.py:51
  314.1 31.2 %all-gather.34 = f32[8,60,128]{2,1,0:T(8,128)S(1)} all-gather(f32[1,60,128]{2,1,0:T(8,128)S(1)} %convolution_bitcast_fusion.29), channel_id=4, replica_groups=mesh['cand'=4,'tp'=8] {'tp'}, dimensions={0}, use_global_device_ids=true | all-gather | bytes 276480 | tf_op jit(solution)/shard_map/all_gather | solution.py:51
  349.3 30.9 %all-gather.35 = f32[8,60,128]{2,1,0:T(8,128)S(1)} all-gather(f32[1,60,128]{2,1,0:T(8,128)S(1)} %convolution_bitcast_fusion.28), channel_id=5, replica_groups=mesh['cand'=4,'tp'=8] {'tp'}, dimensions={0}, use_global_device_ids=true | all-gather | bytes 276480 | tf_op jit(solution)/shard_map/all_gather | solution.py:51
  384.1 30.9 %all-gather.36 = f32[8,60,128]{2,1,0:T(8,128)S(1)} all-gather(f32[1,60,128]{2,1,0:T(8,128)S(1)} %convolution_bitcast_fusion.27), channel_id=6, replica_groups=mesh['cand'=4,'tp'=8] {'tp'}, dimensions={0}, use_global_device_ids=true | all-gather | bytes 276480 | tf_op jit(solution)/shard_map/all_gather | solution.py:51
  418.9 30.9 %all-gather.37 = f32[8,60,128]{2,1,0:T(8,128)S(1)} all-gather(f32[1,60,128]{2,1,0:T(8,128)S(1)} %convolution_bitcast_fusion.26), channel_id=7, replica_groups=mesh['cand'=4,'tp'=8] {'tp'}, dimensions={0}, use_global_device_ids=true | all-gather | bytes 276480 | tf_op jit(solution)/shard_map/all_gather | solution.py:51
  453.7 30.9 %all-gather.38 = f32[8,60,128]{2,1,0:T(8,128)S(1)} all-gather(f32[1,60,128]{2,1,0:T(8,128)S(1)} %convolution_bitcast_fusion.25), channel_id=8, replica_groups=mesh['cand'=4,'tp'=8] {'tp'}, dimensions={0}, use_global_device_ids=true | all-gather | bytes 276480 | tf_op jit(solution)/shard_map/all_gather | solution.py:51
  488.5 30.8 %all-gather.39 = f32[8,60,128]{2,1,0:T(8,128)S(1)} all-gather(f32[1,60,128]{2,1,0:T(8,128)S(1)} %convolution_bitcast_fusion.24), channel_id=9, replica_groups=mesh['cand'=4,'tp'=8] {'tp'}, dimensions={0}, use_global_device_ids=true | all-gather | bytes 276480 | tf_op jit(solution)/shard_map/all_gather | solution.py:51
  519.3 30.8 %all-gather.49 = f32[8,60,128]{2,1,0:T(8,128)S(1)} all-gather(f32[1,60,128]{2,1,0:T(8,128)S(1)} %convolution_bitcast_fusion.14), channel_id=19, replica_groups=mesh['cand'=4,'tp'=8] {'tp'}, dimensions={0}, use_global_device_ids=true | all-gather | bytes 276480 | tf_op jit(solution)/shard_map/all_gather | solution.py:51
  550.1 30.8 %all-gather.42 = f32[8,60,128]{2,1,0:T(8,128)S(1)} all-gather(f32[1,60,128]{2,1,0:T(8,128)S(1)} %convolution_bitcast_fusion.21), channel_id=12, replica_groups=mesh['cand'=4,'tp'=8] {'tp'}, dimensions={0}, use_global_device_ids=true | all-gather | bytes 276480 | tf_op jit(solution)/shard_map/all_gather | solution.py:51
  584.8 30.8 %all-gather.43 = f32[8,60,128]{2,1,0:T(8,128)S(1)} all-gather(f32[1,60,128]{2,1,0:T(8,128)S(1)} %convolution_bitcast_fusion.20), channel_id=13, replica_groups=mesh['cand'=4,'tp'=8] {'tp'}, dimensions={0}, use_global_device_ids=true | all-gather | bytes 276480 | tf_op jit(solution)/shard_map/all_gather | solution.py:51
  619.5 30.8 %all-gather.44 = f32[8,60,128]{2,1,0:T(8,128)S(1)} all-gather(f32[1,60,128]{2,1,0:T(8,128)S(1)} %convolution_bitcast_fusion.19), channel_id=14, replica_groups=mesh['cand'=4,'tp'=8] {'tp'}, dimensions={0}, use_global_device_ids=true | all-gather | bytes 276480 | tf_op jit(solution)/shard_map/all_gather | solution.py:51
  654.1 31.0 %all-gather.45 = f32[8,60,128]{2,1,0:T(8,128)S(1)} all-gather(f32[1,60,128]{2,1,0:T(8,128)S(1)} %convolution_bitcast_fusion.18), channel_id=15, replica_groups=mesh['cand'=4,'tp'=8] {'tp'}, dimensions={0}, use_global_device_ids=true | all-gather | bytes 276480 | tf_op jit(solution)/shard_map/all_gather | solution.py:51
  697.2 30.8 %all-gather.57 = f32[8,60,128]{2,1,0:T(8,128)S(1)} all-gather(f32[1,60,128]{2,1,0:T(8,128)S(1)} %convolution_bitcast_fusion.6), channel_id=27, replica_groups=mesh['cand'=4,'tp'=8] {'tp'}, dimensions={0}, use_global_device_ids=true | all-gather | bytes 276480 | tf_op jit(solution)/shard_map/all_gather | solution.py:51
  731.9 30.8 %all-gather.58 = f32[8,60,128]{2,1,0:T(8,128)S(1)} all-gather(f32[1,60,128]{2,1,0:T(8,128)S(1)} %convolution_bitcast_fusion.5), channel_id=28, replica_groups=mesh['cand'=4,'tp'=8] {'tp'}, dimensions={0}, use_global_device_ids=true | all-gather | bytes 276480 | tf_op jit(solution)/shard_map/all_gather | solution.py:51
  766.5 30.7 %all-gather.59 = f32[8,60,128]{2,1,0:T(8,128)S(1)} all-gather(f32[1,60,128]{2,1,0:T(8,128)S(1)} %convolution_bitcast_fusion.4), channel_id=29, replica_groups=mesh['cand'=4,'tp'=8] {'tp'}, dimensions={0}, use_global_device_ids=true | all-gather | bytes 276480 | tf_op jit(solution)/shard_map/all_gather | solution.py:51
  801.2 30.7 %all-gather.60 = f32[8,60,128]{2,1,0:T(8,128)S(1)} all-gather(f32[1,60,128]{2,1,0:T(8,128)S(1)} %convolution_bitcast_fusion.3), channel_id=30, replica_groups=mesh['cand'=4,'tp'=8] {'tp'}, dimensions={0}, use_global_device_ids=true | all-gather | bytes 276480 | tf_op jit(solution)/shard_map/all_gather | solution.py:51
  835.8 30.9 %all-gather.61 = f32[8,60,128]{2,1,0:T(8,128)S(1)} all-gather(f32[1,60,128]{2,1,0:T(8,128)S(1)} %convolution_bitcast_fusion.2), channel_id=31, replica_groups=mesh['cand'=4,'tp'=8] {'tp'}, dimensions={0}, use_global_device_ids=true | all-gather | bytes 276480 | tf_op jit(solution)/shard_map/all_gather | solution.py:51
  870.6 30.9 %all-gather.62 = f32[8,60,128]{2,1,0:T(8,128)S(1)} all-gather(f32[1,60,128]{2,1,0:T(8,128)S(1)} %convolution_bitcast_fusion.1), channel_id=32, replica_groups=mesh['cand'=4,'tp'=8] {'tp'}, dimensions={0}, use_global_device_ids=true | all-gather | bytes 276480 | tf_op jit(solution)/shard_map/all_gather | solution.py:51
  905.4 30.8 %all-gather.63 = f32[8,60,128]{2,1,0:T(8,128)S(1)} all-gather(f32[1,60,128]{2,1,0:T(8,128)S(1)} %convolution_bitcast_fusion), channel_id=33, replica_groups=mesh['cand'=4,'tp'=8] {'tp'}, dimensions={0}, use_global_device_ids=true | all-gather | bytes 276480 | tf_op jit(solution)/shard_map/all_gather | solution.py:51
  936.2 30.8 %all-gather.50 = f32[8,60,128]{2,1,0:T(8,128)S(1)} all-gather(f32[1,60,128]{2,1,0:T(8,128)S(1)} %convolution_bitcast_fusion.13), channel_id=20, replica_groups=mesh['cand'=4,'tp'=8] {'tp'}, dimensions={0}, use_global_device_ids=true | all-gather | bytes 276480 | tf_op jit(solution)/shard_map/all_gather | solution.py:51
  970.9 30.9 %all-gather.51 = f32[8,60,128]{2,1,0:T(8,128)S(1)} all-gather(f32[1,60,128]{2,1,0:T(8,128)S(1)} %convolution_bitcast_fusion.12), channel_id=21, replica_groups=mesh['cand'=4,'tp'=8] {'tp'}, dimensions={0}, use_global_device_ids=true | all-gather | bytes 276480 | tf_op jit(solution)/shard_map/all_gather | solution.py:51
  1005.7 31.0 %all-gather.52 = f32[8,60,128]{2,1,0:T(8,128)S(1)} all-gather(f32[1,60,128]{2,1,0:T(8,128)S(1)} %convolution_bitcast_fusion.11), channel_id=22, replica_groups=mesh['cand'=4,'tp'=8] {'tp'}, dimensions={0}, use_global_device_ids=true | all-gather | bytes 276480 | tf_op jit(solution)/shard_map/all_gather | solution.py:51
  1040.5 30.7 %all-gather.53 = f32[8,60,128]{2,1,0:T(8,128)S(1)} all-gather(f32[1,60,128]{2,1,0:T(8,128)S(1)} %convolution_bitcast_fusion.10), channel_id=23, replica_groups=mesh['cand'=4,'tp'=8] {'tp'}, dimensions={0}, use_global_device_ids=true | all-gather | bytes 276480 | tf_op jit(solution)/shard_map/all_gather | solution.py:51
  1075.2 30.7 %all-gather.54 = f32[8,60,128]{2,1,0:T(8,128)S(1)} all-gather(f32[1,60,128]{2,1,0:T(8,128)S(1)} %convolution_bitcast_fusion.9), channel_id=24, replica_groups=mesh['cand'=4,'tp'=8] {'tp'}, dimensions={0}, use_global_device_ids=true | all-gather | bytes 276480 | tf_op jit(solution)/shard_map/all_gather | solution.py:51
  1140.6 30.7 %all-gather.46 = f32[8,60,128]{2,1,0:T(8,128)S(1)} all-gather(f32[1,60,128]{2,1,0:T(8,128)S(1)} %convolution_bitcast_fusion.17), channel_id=16, replica_groups=mesh['cand'=4,'tp'=8] {'tp'}, dimensions={0}, use_global_device_ids=true | all-gather | bytes 276480 | tf_op jit(solution)/shard_map/all_gather | solution.py:51
  1175.3 30.7 %all-gather.47 = f32[8,60,128]{2,1,0:T(8,128)S(1)} all-gather(f32[1,60,128]{2,1,0:T(8,128)S(1)} %convolution_bitcast_fusion.16), channel_id=17, replica_groups=mesh['cand'=4,'tp'=8] {'tp'}, dimensions={0}, use_global_device_ids=true | all-gather | bytes 276480 | tf_op jit(solution)/shard_map/all_gather | solution.py:51
  (214 shorter events, 197.7 us)
Async XLA Ops:
  7.2 86.2 %all-gather.66.cloned.1.call-start = ((), (), s32[]{:S(2)}) async-start(), calls=%async_computation | async-start | bytes 5308416 | tf_op jit(solution)/shard_map/all_gather | solution.py:29
  93.4 3.7 copy-start
  105.0 65.8 %copy-start.2 = (f32[128]{0:T(128)S(1)}, f32[128]{0:T(128)}, u32[]{:S(2)}) copy-start(f32[128]{0:T(128)} %param.10) | copy-start | bytes 1540
  650.3 34.9 %copy-start.5 = (f32[128]{0:T(128)S(1)}, f32[128]{0:T(128)}, u32[]{:S(2)}) copy-start(f32[128]{0:T(128)} %param.11) | copy-start | bytes 1540
  1171.3 43.6 %copy-start.7 = (s32[96]{0:T(128)S(1)}, s32[96]{0:T(128)}, u32[]{:S(2)}) copy-start(s32[96]{0:T(128)} %param.16) | copy-start | bytes 1156
  1171.4 53.0 %copy-start.1 = (f32[192,128]{1,0:T(8,128)S(1)}, f32[192,128]{1,0:T(8,128)}, u32[]{:S(2)}) copy-start(f32[192,128]{1,0:T(8,128)} %param.14) | copy-start | bytes 294916
  1171.4 53.0 %copy-start.3 = (f32[128]{0:T(128)S(1)}, f32[128]{0:T(128)}, u32[]{:S(2)}) copy-start(f32[128]{0:T(128)} %param.13) | copy-start | bytes 1540
  1171.4 53.0 %copy-start.4 = (f32[128]{0:T(128)S(1)}, f32[128]{0:T(128)}, u32[]{:S(2)}) copy-start(f32[128]{0:T(128)} %param.12) | copy-start | bytes 1540
  1231.8 7.4 copy-start.6
Sparse Core Ops, SparseCore 0:
  10.0 83.3 all-gather.65
